TPU v7x, 32 devices: a whole 2x2x4 slice. The times are simulated.
32 devices in a mesh: path: 4 (over z), tm: 8 (over y, x, core).
Axes of the slice: x: 2, y: 2, z: 4, core: 2. Of those that a mesh axis runs over, the one named last changes fastest.
Arguments:
- values: bfloat16 [2048, 16, 2048], P('path', 'tm'), may hold values from -5 to 5
- hazard: float32 [16, 2048], P('tm', 'path'), may hold values from 0.0125 to 0.1875
- spread: float32 [16], P('tm'), may hold values from 0.3 to 3
- trade_set: int32 [2048], replicated, may hold values from 0 to 255
Outputs:
- pathwise_fva: float32 [2048, 256], P(('path', 'tm'))
- set_fva: float32 [256], P(('path', 'tm'))
All inputs are finite; a program needn't handle non-finite values.
Results may differ from a plain program's by a relative error of at most 0.0003.
Values sent between devices are 32-bit elements; how exact they have to be, the bound alone decides.
A program may use at most 64 MiB of HBM per device.

v0:
```python
import jax
import jax.numpy as jnp
from jax import lax
from jax.sharding import PartitionSpec as P

SETS = 256


def on_device(values, hazard, spread, trade_set):
    paths_dev, dates_dev, trades = values.shape
    dates_total = dates_dev * lax.axis_size("tm")
    paths_total = paths_dev * lax.axis_size("path")
    onehot = (trade_set[:, None] == jnp.arange(SETS, dtype=jnp.int32)[None, :]).astype(jnp.bfloat16)
    netted = jnp.dot(
        values.reshape(paths_dev * dates_dev, trades), onehot, preferred_element_type=jnp.float32
    )
    positive = jnp.maximum(netted.reshape(paths_dev, dates_dev, SETS), 0.0)
    survival = jnp.exp(-jnp.cumsum(hazard, axis=0))
    block_product = survival[-1]
    weights = jnp.transpose(spread[:, None] * survival)
    local_sum = jnp.einsum("pt,pts->ps", weights, positive, precision=lax.Precision.HIGHEST)
    gathered_sums, gathered_products = (
        lax.all_to_all(local_sum[None], "tm", split_axis=1, concat_axis=0, tiled=True),
        lax.all_to_all(block_product[None], "tm", split_axis=1, concat_axis=0, tiled=True),
    )
    earlier = jnp.concatenate(
        [jnp.ones_like(gathered_products[:1]), jnp.cumprod(gathered_products[:-1], axis=0)], axis=0
    )
    shares = jnp.einsum("kp,kps->ps", earlier, gathered_sums, precision=lax.Precision.HIGHEST)
    pathwise_fva = shares / dates_total
    set_part = jnp.sum(pathwise_fva, axis=0) / paths_total
    set_fva = lax.psum_scatter(set_part, ("path", "tm"), scatter_dimension=0, tiled=True)
    return (pathwise_fva, set_fva)


def solution(mesh):
    in_specs = (P("path", "tm", None), P("tm", "path"), P("tm"), P())
    out_specs = (P(("path", "tm"), None), P(("path", "tm")))
    return jax.shard_map(
        on_device, mesh=mesh, in_specs=in_specs, out_specs=out_specs, check_vma=False
    )
```

profile of v0, /device:TPU:0, one launch (start us, length us, event | category | flops | bytes accessed | tf_op | source)
XLA Modules:
  0.0 80.7 jit_solution(11877485971977223632)
XLA Ops:
  0.6 0.7 reduce_window_sum.11
  1.3 0.7 multiply_bitcast_fusion
  2.1 0.7 all_to_all.9
  2.8 5.2 %all-to-all-start = ((f32[1,8,64]{2,0,1:T(1,128)}), f32[1,8,64]{2,0,1:T(1,128)S(1)}, u32[]{:S(2)}, u32[]{:S(2)}) async-start(f32[1,8,64]{2,0,1:T(1,128)} %all_to_all.9), calls=%async_computation | async-start | bytes 8192 | tf_op jit(solution)/shard_map/all_to_all | solution.py:24
  8.0 0.1 copy.8
  8.1 0.0 copy-start
  8.1 7.2 %reshape.21 = bf16[1024,2048]{1,0:T(8,128)(2,1)} reshape(bf16[512,2,2048]{2,1,0:T(2,128)(2,1)} %param.4) | data formatting | bytes 8388608 | tf_op jit(solution)/shard_map/reshape | solution.py:15
  15.4 0.0 copy-done
  15.4 3.8 %fusion.1 = f32[1024,256]{0,1:T(8,128)S(1)} fusion(bf16[1024,2048]{1,0:T(8,128)(2,1)} %reshape.21, s32[2048]{0:T(1024)S(1)} %copy-done), kind=kOutput, calls=%fused_computation.3 | convolution fusion | flops 1075052544 | bytes 5251072 | tf_op jit(solution)/shard_map/dot_general | solution.py:14
  19.2 0.3 copy.7
  19.6 0.6 max.15
  20.2 3.8 %fusion.7 = f32[512,1,256]{2,1,0:T(1,128)S(1)} fusion(f32[512,2,1]{1,2,0:T(1,128)S(1)} %copy.8, f32[512,2,256]{2,1,0:T(2,128)S(1)} %max.15), kind=kOutput, calls=%fused_computation.16 | convolution fusion | flops 3145728 | bytes 1576960 | tf_op jit(solution)/shard_map/pt,pts->ps/dot_general | solution.py:21
  24.1 1.1 %broadcast_in_dim.2 = f32[1,512,256]{2,0,1:T(1,128)} reshape(f32[512,256]{1,0:T(8,128)S(1)} %bitcast.23) | data formatting | bytes 1048576 | tf_op jit(solution)/shard_map/broadcast_in_dim | solution.py:23
  25.2 0.0 all-to-all-done
  25.2 4.2 %all-to-all-start.1 = ((f32[1,512,256]{2,0,1:T(1,128)}), f32[1,512,256]{2,0,1:T(1,128)S(1)}, u32[]{:S(2)}, u32[]{:S(2)}) async-start(f32[1,512,256]{2,0,1:T(1,128)} %broadcast_in_dim.2), calls=%async_computation.1 | async-start | bytes 1048576 | tf_op jit(solution)/shard_map/all_to_all | solution.py:23
  29.5 0.1 copy.10
  29.6 9.6 %all-to-all-done.1 = f32[1,512,256]{2,0,1:T(1,128)S(1)} async-done(((f32[1,512,256]{2,0,1:T(1,128)}), f32[1,512,256]{2,0,1:T(1,128)S(1)}, u32[]{:S(2)}, u32[]{:S(2)}) %all-to-all-start.1) | async-done | bytes 524320 | tf_op jit(solution)/shard_map/all_to_all | solution.py:23
  39.2 0.9 %fusion.4 = f32[64,1,256]{2,1,0:T(1,128)S(1)} fusion(f32[8,64,1]{0,2,1:T(1,128)S(1)} %copy.10, f32[8,64,256]{2,1,0:T(8,128)S(1)} %bitcast.22), kind=kOutput, calls=%fused_computation.5 | convolution fusion | flops 1572864 | bytes 591872 | tf_op jit(solution)/shard_map/kp,kps->ps/dot_general | solution.py:29
  40.0 0.6 fusion.6
  40.7 39.4 %all-reduce.1 = f32[256]{0:T(256)S(1)} all-reduce(f32[256]{0:T(256)S(1)} %broadcast_multiply_fusion), channel_id=2, replica_groups=mesh['path'=4,'tm'=8] {'path','tm'}, use_global_device_ids=true, to_apply=%region_3.4.clone | all-reduce | flops 256 | bytes 2048
  80.1 0.6 dynamic-slice
  (8 shorter events, 0.1 us)
Async XLA Ops:
  2.8 22.5 %all-to-all-start = ((f32[1,8,64]{2,0,1:T(1,128)}), f32[1,8,64]{2,0,1:T(1,128)S(1)}, u32[]{:S(2)}, u32[]{:S(2)}) async-start(f32[1,8,64]{2,0,1:T(1,128)} %all_to_all.9), calls=%async_computation | async-start | bytes 8192 | tf_op jit(solution)/shard_map/all_to_all | solution.py:24
  8.1 7.2 %copy-start = (s32[2048]{0:T(1024)S(1)}, s32[2048]{0:T(1024)}, u32[]{:S(2)}) copy-start(s32[2048]{0:T(1024)} %param.7) | copy-start | bytes 24580
  25.2 13.9 %all-to-all-start.1 = ((f32[1,512,256]{2,0,1:T(1,128)}), f32[1,512,256]{2,0,1:T(1,128)S(1)}, u32[]{:S(2)}, u32[]{:S(2)}) async-start(f32[1,512,256]{2,0,1:T(1,128)} %broadcast_in_dim.2), calls=%async_computation.1 | async-start | bytes 1048576 | tf_op jit(solution)/shard_map/all_to_all | solution.py:23
where the time goes:
time: 81.2 us; the launch traced here: 80.7 us
  blocking collectives  39.4 us (49%)
  local copies, waits for them, and re-layouts  10.9 us (13%)
  waiting for transfers between devices  9.58 us (12%)
  starting transfers between devices  9.4 us (12%)
  matrix products  8.55 us (11%)
  other arithmetic  2.11 us (3%)
    unnamed x1, blocking collectives  39.4 us
    all_to_all x1, waiting for transfers between devices, on_device(): lax.all_to_all(local_sum[None], 'tm', split_axis=1, concat_axis=0, tiled=...  9.57 us
    reshape x1, local copies, waits for them, and re-layouts, on_device(): values.reshape(paths_dev * dates_dev, trades)  7.22 us
    all_to_all x1, starting transfers between devices, on_device(): lax.all_to_all(block_product[None], 'tm', split_axis=1, concat_axis=0, ti...  5.2 us
    all_to_all x1, starting transfers between devices, on_device(): lax.all_to_all(local_sum[None], 'tm', split_axis=1, concat_axis=0, tiled=...  4.2 us
    dot_general x1, matrix products, on_device(): jnp.dot(values.reshape(paths_dev * dates_dev, trades), onehot, preferred_...  3.85 us
    dot_general x1, matrix products, on_device(): jnp.einsum('pt,pts->ps', weights, positive, precision=lax.Precision.HIGHEST)  3.85 us
  transfers between devices with their start and end apart: 2, of which 1 were waited for; matrix products, arithmetic and copies ran while one was open for 21% of the time, Pallas kernels for 0%

commit v1 on v0

--- a/solution.py
+++ b/solution.py
@@ -21,7 +21,12 @@
     local_sum = jnp.einsum("pt,pts->ps", weights, positive, precision=lax.Precision.HIGHEST)
     gathered_sums, gathered_products = (
         lax.all_to_all(local_sum[None], "tm", split_axis=1, concat_axis=0, tiled=True),
-        lax.all_to_all(block_product[None], "tm", split_axis=1, concat_axis=0, tiled=True),
+        jnp.concatenate(
+            lax.all_to_all(
+                jnp.stack(jnp.split(block_product[None], lax.axis_size("tm"), axis=1)), "tm", 0, 0
+            ),
+            axis=0,
+        ),
     )
     earlier = jnp.concatenate(
         [jnp.ones_like(gathered_products[:1]), jnp.cumprod(gathered_products[:-1], axis=0)], axis=0

time: 81.2 us -> 84.9 us (1.046)
  local copies, waits for them, and re-layouts: 10.9 us -> 14.6 us
    unnamed x5 -> x12, local copies, waits for them, and re-layouts: 0.63 us -> 4.42 us
where the time goes in v1:
time: 84.9 us; the launch traced here: 84.3 us
  blocking collectives  39.4 us (46%)
  local copies, waits for them, and re-layouts  14.6 us (17%)
  waiting for transfers between devices  9.58 us (11%)
  starting transfers between devices  9.38 us (11%)
  matrix products  8.57 us (10%)
  other arithmetic  2.11 us (2%)
    unnamed x1, blocking collectives  39.4 us
    all_to_all x1, waiting for transfers between devices, on_device(): lax.all_to_all(local_sum[None], 'tm', split_axis=1, concat_axis=0, tiled=...  9.57 us
    reshape x1, local copies, waits for them, and re-layouts, on_device(): values.reshape(paths_dev * dates_dev, trades)  7.22 us
    all_to_all x1, starting transfers between devices, on_device(): lax.all_to_all(jnp.stack(jnp.split(block_product[None], lax.axis_size('tm...  5.2 us
    unnamed x12, local copies, waits for them, and re-layouts  4.42 us
    all_to_all x1, starting transfers between devices, on_device(): lax.all_to_all(local_sum[None], 'tm', split_axis=1, concat_axis=0, tiled=...  4.18 us
    dot_general x1, matrix products, on_device(): jnp.dot(values.reshape(paths_dev * dates_dev, trades), onehot, preferred_...  3.87 us
    dot_general x1, matrix products, on_device(): jnp.einsum('pt,pts->ps', weights, positive, precision=lax.Precision.HIGHEST)  3.85 us
  transfers between devices with their start and end apart: 2, of which 1 were waited for; matrix products, arithmetic and copies ran while one was open for 21% of the time, Pallas kernels for 0%

profile of v1, /device:TPU:0, one launch (start us, length us, event | category | flops | bytes accessed | tf_op | source)
XLA Modules:
  0.0 84.3 jit_solution(13043413894317564552)
XLA Ops:
  0.6 0.7 reduce_window_sum.11
  1.3 0.7 multiply_bitcast_fusion
  2.1 0.5 constant_dynamic-update-slice_fusion.7
  2.6 0.6 constant_dynamic-update-slice_fusion.6
  3.2 0.5 constant_dynamic-update-slice_fusion.5
  3.7 0.6 constant_dynamic-update-slice_fusion.4
  4.3 0.5 constant_dynamic-update-slice_fusion.3
  4.8 0.6 constant_dynamic-update-slice_fusion.2
  5.4 0.5 constant_dynamic-update-slice_fusion.1
  5.9 0.6 constant_dynamic-update-slice_fusion
  6.4 5.2 %all-to-all-start = ((f32[8,1,64]{2,1,0:T(1,128)}), f32[8,1,64]{2,1,0:T(1,128)S(1)}, u32[]{:S(2)}, u32[]{:S(2)}) async-start(f32[8,1,64]{2,1,0:T(1,128)} %constant_dynamic-update-slice_fusion), calls=%async_computation | async-start | bytes 8192 | tf_op jit(solution)/shard_map/all_to_all | solution.py:25
  11.6 0.1 copy.8
  11.8 0.0 copy-start
  11.8 7.2 %reshape.17 = bf16[1024,2048]{1,0:T(8,128)(2,1)} reshape(bf16[512,2,2048]{2,1,0:T(2,128)(2,1)} %param.4) | data formatting | bytes 8388608 | tf_op jit(solution)/shard_map/reshape | solution.py:15
  19.0 0.0 copy-done
  19.0 3.9 %fusion.1 = f32[1024,256]{0,1:T(8,128)S(1)} fusion(bf16[1024,2048]{1,0:T(8,128)(2,1)} %reshape.17, s32[2048]{0:T(1024)S(1)} %copy-done), kind=kOutput, calls=%fused_computation.3 | convolution fusion | flops 1075052544 | bytes 5251072 | tf_op jit(solution)/shard_map/dot_general | solution.py:14
  22.9 0.3 copy.7
  23.2 0.6 max.15
  23.9 3.8 %fusion.7 = f32[512,1,256]{2,1,0:T(1,128)S(1)} fusion(f32[512,2,1]{1,2,0:T(1,128)S(1)} %copy.8, f32[512,2,256]{2,1,0:T(2,128)S(1)} %max.15), kind=kOutput, calls=%fused_computation.31 | convolution fusion | flops 3145728 | bytes 1576960 | tf_op jit(solution)/shard_map/pt,pts->ps/dot_general | solution.py:21
  27.8 1.1 %broadcast_in_dim.2 = f32[1,512,256]{2,0,1:T(1,128)} reshape(f32[512,256]{1,0:T(8,128)S(1)} %bitcast.55) | data formatting | bytes 1048576 | tf_op jit(solution)/shard_map/broadcast_in_dim | solution.py:23
  28.9 0.0 all-to-all-done
  28.9 4.2 %all-to-all-start.1 = ((f32[1,512,256]{2,0,1:T(1,128)}), f32[1,512,256]{2,0,1:T(1,128)S(1)}, u32[]{:S(2)}, u32[]{:S(2)}) async-start(f32[1,512,256]{2,0,1:T(1,128)} %broadcast_in_dim.2), calls=%async_computation.1 | async-start | bytes 1048576 | tf_op jit(solution)/shard_map/all_to_all | solution.py:23
  33.2 0.1 copy.10
  33.2 9.6 %all-to-all-done.1 = f32[1,512,256]{2,0,1:T(1,128)S(1)} async-done(((f32[1,512,256]{2,0,1:T(1,128)}), f32[1,512,256]{2,0,1:T(1,128)S(1)}, u32[]{:S(2)}, u32[]{:S(2)}) %all-to-all-start.1) | async-done | bytes 524320 | tf_op jit(solution)/shard_map/all_to_all | solution.py:23
  42.9 0.9 %fusion.4 = f32[64,1,256]{2,1,0:T(1,128)S(1)} fusion(f32[8,64,1]{0,2,1:T(1,128)S(1)} %copy.10, f32[8,64,256]{2,1,0:T(8,128)S(1)} %bitcast.54), kind=kOutput, calls=%fused_computation.5 | convolution fusion | flops 1572864 | bytes 591872 | tf_op jit(solution)/shard_map/kp,kps->ps/dot_general | solution.py:34
  43.7 0.6 fusion.6
  44.4 39.4 %all-reduce.1 = f32[256]{0:T(256)S(1)} all-reduce(f32[256]{0:T(256)S(1)} %broadcast_multiply_fusion), channel_id=2, replica_groups=mesh['path'=4,'tm'=8] {'path','tm'}, use_global_device_ids=true, to_apply=%region_3.4.clone | all-reduce | flops 256 | bytes 2048
  83.8 0.6 dynamic-slice
  (7 shorter events, 0.1 us)
Async XLA Ops:
  6.4 22.5 %all-to-all-start = ((f32[8,1,64]{2,1,0:T(1,128)}), f32[8,1,64]{2,1,0:T(1,128)S(1)}, u32[]{:S(2)}, u32[]{:S(2)}) async-start(f32[8,1,64]{2,1,0:T(1,128)} %constant_dynamic-update-slice_fusion), calls=%async_computation | async-start | bytes 8192 | tf_op jit(solution)/shard_map/all_to_all | solution.py:25
  11.8 7.2 %copy-start = (s32[2048]{0:T(1024)S(1)}, s32[2048]{0:T(1024)}, u32[]{:S(2)}) copy-start(s32[2048]{0:T(1024)} %param.7) | copy-start | bytes 24580
  28.9 13.9 %all-to-all-start.1 = ((f32[1,512,256]{2,0,1:T(1,128)}), f32[1,512,256]{2,0,1:T(1,128)S(1)}, u32[]{:S(2)}, u32[]{:S(2)}) async-start(f32[1,512,256]{2,0,1:T(1,128)} %broadcast_in_dim.2), calls=%async_computation.1 | async-start | bytes 1048576 | tf_op jit(solution)/shard_map/all_to_all | solution.py:23
